TPU v7x, 32 devices: a whole 2x2x4 slice. The times are simulated.
32 devices in a mesh: band: 8 (over z, x), sub: 4 (over y, core).
Axes of the slice: x: 2, y: 2, z: 4, core: 2. Of those that a mesh axis runs over, the one named last changes fastest.
Arguments:
- grad_pred: bfloat16 [227, 24576], P(None, ('band', 'sub')), may hold values from -6 to 6
- grid_latent: bfloat16 [24576, 512], P(('band', 'sub')), may hold values from -6 to 6
- mesh_latent: bfloat16 [10240, 512], P(('band', 'sub')), may hold values from -6 to 6
- send_slot: int32 [24576], P(('band', 'sub')), may hold values from 0 to 2303, as said below
- edge_src: int32 [3, 73728], P(None, ('band', 'sub')), may hold values from 0 to 10239, as said below
- w_mesh: bfloat16 [512, 512], replicated, may hold values from -0.25 to 0.25
- w_grid: bfloat16 [512, 512], replicated, may hold values from -0.25 to 0.25
- w_msg: bfloat16 [512, 512], replicated, may hold values from -0.25 to 0.25
- w_out: bfloat16 [512, 227], replicated, may hold values from -0.25 to 0.25
Outputs:
- mesh_grad: bfloat16 [10240, 512], P(('band', 'sub'))
- grad_w_mesh: float32 [512, 512], replicated
- grad_w_grid: float32 [512, 512], replicated
- grad_w_msg: float32 [512, 512], replicated
- grad_w_out: float32 [512, 227], replicated
Inputs may be any that keep to these rules, and one draw needn't show every extreme that they name: For grid point p on latitude-major device i, send_slot[p] = j * 72 + r names patch-major device j and a rank r. On one device i the values are distinct, and for each j the ranks used are 0 to the count of i's points sent to j minus 1. Every such count is at most 72, and 72 is reached in every draw. Every grid point thereby gets one patch-major slot; live slots of each source stand at the front of its block of 72. One patch-major device holds at most 1920 live slots, reached on some device in every draw. `edge_src`: A slot on patch-major device j, of band b = j // 4, names senders in patch b only: mesh rows b * 1280 to (b + 1) * 1280 - 1. Entries of empty slots lie in that range too and are not read.
All inputs are finite; a program needn't handle non-finite values.
Results may differ from a plain program's by a relative error of at most 0.0076.
Values may be sent and summed in bfloat16 or wider, within the bound.
No kernel may reach another device: no remote copies, remote signals or barrier semaphores. Data moves between devices by JAX's collectives and lax.ppermute only.
A program may use at most 128 MiB of HBM per device.

v0:
```python
import math
import jax
import jax.numpy as jnp
from jax import lax
from jax.sharding import PartitionSpec as P


def latitude_weight(points, total):
    angle = jnp.pi * ((points.astype(jnp.float32) + 0.5) / total - 0.5)
    return 0.5 * jnp.pi * jnp.cos(angle)


def silu_slope(value):
    sigma = jax.nn.sigmoid(value)
    return sigma * (1.0 + value * (1.0 - sigma))


def contract_rows(left, right):
    return lax.dot_general(
        left, right, (((0,), (0,)), ((), ())), preferred_element_type=jnp.float32
    )


def times_transpose(left, right):
    return lax.dot_general(
        left, right, (((1,), (1,)), ((), ())), preferred_element_type=jnp.float32
    )


def shards(grad_pred, grid_latent, mesh_latent, send_slot, edge_src, w_mesh, w_grid, w_msg, w_out):
    grid_rows = grid_latent.shape[0]
    width = grid_latent.shape[1]
    channels = grad_pred.shape[0]
    devices = lax.axis_size(("band", "sub"))
    capacity = 3 * grid_rows // devices
    total_points = grid_rows * devices
    own_index = lax.axis_index(("band", "sub"))
    points = own_index * grid_rows + jnp.arange(grid_rows, dtype=jnp.int32)
    weighted = (
        latitude_weight(points, total_points)[None, :] * grad_pred.astype(jnp.float32)
    ).astype(jnp.bfloat16)
    target = send_slot // capacity
    slot_rank = send_slot % capacity
    joined = jnp.concatenate([grid_latent, weighted.T], axis=1)
    row_width = width + channels
    send_buffer = (
        jnp.zeros((devices, capacity, row_width), jnp.bfloat16).at[target, slot_rank].set(joined)
    )
    received = lax.all_to_all(send_buffer, ("band", "sub"), split_axis=0, concat_axis=0, tiled=True)
    slots = devices * capacity
    slot_rows = received.reshape(slots, row_width)
    latent_rows = slot_rows[:, :width]
    grad_rows = slot_rows[:, width:]
    grid_proj = jnp.dot(latent_rows, w_grid, preferred_element_type=jnp.float32).astype(
        jnp.bfloat16
    )
    mesh_proj = jnp.dot(mesh_latent, w_mesh, preferred_element_type=jnp.float32).astype(
        jnp.bfloat16
    )
    patch_proj = lax.all_gather(mesh_proj, "sub", axis=0, tiled=True)
    patch_size = patch_proj.shape[0]
    band_index = lax.axis_index("band")
    local_node = edge_src - band_index * patch_size
    grid_float = grid_proj.astype(jnp.float32)
    pre_acts = [
        patch_proj[local_node[corner]].astype(jnp.float32) + grid_float for corner in range(3)
    ]
    act_sum = (
        jax.nn.silu(pre_acts[0]) + jax.nn.silu(pre_acts[1]) + jax.nn.silu(pre_acts[2])
    ).astype(jnp.bfloat16)
    aggregate = jnp.dot(act_sum, w_msg, preferred_element_type=jnp.float32).astype(jnp.bfloat16)
    out_part = contract_rows(aggregate, grad_rows)
    agg_rows = times_transpose(grad_rows, w_out).astype(jnp.bfloat16)
    msg_part = contract_rows(act_sum, agg_rows)
    out_total = lax.psum(out_part, ("band", "sub"))
    msg_total = lax.psum(msg_part, ("band", "sub"))
    act_grad = times_transpose(agg_rows, w_msg)
    pre_grads = [(act_grad * silu_slope(pre)).astype(jnp.bfloat16) for pre in pre_acts]
    grid_proj_grad = (
        pre_grads[0].astype(jnp.float32)
        + pre_grads[1].astype(jnp.float32)
        + pre_grads[2].astype(jnp.float32)
    ).astype(jnp.bfloat16)
    node_part = jnp.zeros((patch_size, width), jnp.float32)
    for corner in range(3):
        node_part = node_part.at[local_node[corner]].add(pre_grads[corner].astype(jnp.float32))
    node_total = lax.psum_scatter(node_part, "sub", scatter_dimension=0, tiled=True)
    grid_part = contract_rows(latent_rows, grid_proj_grad)
    mesh_proj_grad = node_total.astype(jnp.bfloat16)
    mesh_grad = times_transpose(mesh_proj_grad, w_mesh).astype(jnp.bfloat16)
    mesh_part = contract_rows(mesh_latent, mesh_proj_grad)
    grad_scale = 1.0 / math.sqrt(3.0 * total_points)
    grid_total = lax.psum(grid_part, ("band", "sub"))
    mesh_total = lax.psum(mesh_part, ("band", "sub"))
    return (
        mesh_grad,
        mesh_total * grad_scale,
        grid_total * grad_scale,
        msg_total * grad_scale,
        out_total * grad_scale,
    )


def solution(mesh):
    placed = (
        P(None, ("band", "sub")),
        P(("band", "sub"), None),
        P(("band", "sub"), None),
        P(("band", "sub")),
        P(None, ("band", "sub")),
        P(),
        P(),
        P(),
        P(),
    )
    return jax.shard_map(
        shards,
        mesh=mesh,
        in_specs=placed,
        out_specs=(P(("band", "sub"), None), P(), P(), P(), P()),
        check_vma=False,
    )
```

profile of v0, /device:TPU:0, one launch (start us, length us, event | category | flops | bytes accessed | tf_op | source)
XLA Modules:
  0.0 467.4 jit_solution(4389432427457058807)
XLA Ops:
  7.2 0.0 copy-start
  7.2 0.8 compare_select_fusion.4
  8.0 1.0 fusion.15
  9.0 0.2 copy.26
  9.2 1.2 pad_maximum_fusion
  10.5 2.0 broadcast_in_dim.9
  12.5 101.6 %scatter_fusion = bf16[32,72,739]{2,1,0:T(8,128)(2,1)} fusion(bf16[32,72,739]{2,1,0:T(8,128)(2,1)} %broadcast_in_dim.9, s32[768]{0:T(1024)S(1)} %fusion.23, bf16[768,739]{1,0:T(8,128)(2,1)S(1)} %pad_maximum_fusion), kind=kCustom, calls=%fused_computation.3 | custom fusion | bytes 3411456 | tf_op jit(solution)/shard_map/scatter | solution.py:47
  114.1 7.4 %all-to-all-start = ((bf16[32,72,739]{2,1,0:T(8,128)(2,1)}), bf16[32,72,739]{2,1,0:T(8,128)(2,1)}, u32[]{:S(2)}, u32[]{:S(2)}) async-start(bf16[32,72,739]{2,1,0:T(8,128)(2,1)} %scatter_fusion), calls=%async_computation | async-start | bytes 7077888 | tf_op jit(solution)/shard_map/all_to_all | solution.py:49
  121.6 0.0 all-gather.2.cloned.1.call-start
  121.6 1.1 convolution_convert_fusion.4
  122.7 0.0 all-gather.2.cloned.1.call-update
  122.7 0.0 reduce-scatter.2.cloned.1.call-start
  122.8 0.1 fusion.20
  122.9 33.9 %all-gather.2.cloned.1.call-done = bf16[1280,512]{1,0:T(8,128)(2,1)} async-done(((bf16[320,512]{1,0:T(8,128)(2,1)}), bf16[1280,512]{1,0:T(8,128)(2,1)}) %all-gather.2.cloned.1.call-update) | async-done | bytes 1310736 | tf_op jit(solution)/shard_map/all_gather | solution.py:60
  156.9 9.2 %gather_fusion.2 = bf16[2304,512]{1,0:T(8,128)(2,1)} fusion(bf16[1280,512]{1,0:T(8,128)(2,1)} %all-gather.2.cloned.1.call-done, s32[3072]{0:T(1024)S(1)} %get-tuple-element.33), kind=kCustom, calls=%fused_computation.2 | custom fusion | bytes 4727808 | tf_op jit(solution)/shard_map/gather | solution.py:66
  166.1 7.5 %gather_fusion.1 = bf16[2304,512]{1,0:T(8,128)(2,1)} fusion(bf16[1280,512]{1,0:T(8,128)(2,1)S(1)} %copy-done.1, s32[3072]{0:T(1024)S(1)} %get-tuple-element.34), kind=kCustom, calls=%fused_computation.1 | custom fusion | bytes 4727808 | tf_op jit(solution)/shard_map/gather | solution.py:66
  173.6 7.5 %gather_fusion = bf16[2304,512]{1,0:T(8,128)(2,1)} fusion(bf16[1280,512]{1,0:T(8,128)(2,1)S(1)} %copy-done.1, s32[3072]{0:T(1024)S(1)} %pad_clamp_fusion.2), kind=kCustom, calls=%fused_computation | custom fusion | bytes 4727808 | tf_op jit(solution)/shard_map/gather | solution.py:66
  181.1 20.5 %all-to-all-done = bf16[32,72,739]{2,1,0:T(8,128)(2,1)} async-done(((bf16[32,72,739]{2,1,0:T(8,128)(2,1)}), bf16[32,72,739]{2,1,0:T(8,128)(2,1)}, u32[]{:S(2)}, u32[]{:S(2)}) %all-to-all-start) | async-done | bytes 3405344 | tf_op jit(solution)/shard_map/all_to_all | solution.py:49
  201.6 2.0 convolution_convert_fusion.2
  203.7 3.9 convolution_convert_fusion.1
  207.7 0.0 copy-done.5
  207.7 0.0 copy-done
  207.7 0.0 copy-done.6
  207.7 0.0 copy-done.7
  207.7 0.6 copy-done.8
  208.4 9.1 %multiply_convert_fusion = (bf16[2304,512]{1,0:T(8,128)(2,1)}, bf16[2304,512]{1,0:T(8,128)(2,1)}, bf16[2304,512]{1,0:T(8,128)(2,1)}, bf16[2304,512]{1,0:T(8,128)(2,1)}) fusion(bf16[2304,512]{1,0:T(8,128)(2,1)S(1)} %convolution_convert_fusion.1, bf16[2304,512]{1,0:T(8,128)(2,1)S(1)} %copy-done.6, bf16[2304,512]{1,0:T(8,128)(2,1)S(1)} %copy-done.7, ...), kind=kOutput, calls=%fused_computation.20 | convolution fusion | flops 1255145472 | bytes 21757952 | tf_op jit(solution)/shard_map/dot_general | solution.py:25
  217.4 17.0 %scatter_custom_fusion.1 = f32[1280,512]{1,0:T(8,128)S(1)} fusion(s32[2304]{0:T(1024)S(1)} %get-tuple-element.22, bf16[2304,512]{1,0:T(8,128)(2,1)} %get-tuple-element.30, f32[]{:T(128)} %constant.20.clone.1), kind=kCustom, calls=%fused_computation.16 | custom fusion | flops 2359296 | bytes 4980740 | tf_op jit(solution)/shard_map/scatter-add | solution.py:86
  234.5 17.5 %scatter_custom_fusion.2 = f32[1280,512]{1,0:T(8,128)S(1)} fusion(f32[1280,512]{1,0:T(8,128)S(1)} %scatter_custom_fusion.1, s32[2304]{0:T(1024)S(1)} %get-tuple-element.21, bf16[2304,512]{1,0:T(8,128)(2,1)} %get-tuple-element.28), kind=kCustom, calls=%fused_computation.14 | custom fusion | flops 2359296 | bytes 4980736 | tf_op jit(solution)/shard_map/scatter-add | solution.py:86
  252.0 17.4 %scatter_custom_fusion.3 = f32[1280,512]{1,0:T(8,128)S(1)} fusion(f32[1280,512]{1,0:T(8,128)S(1)} %scatter_custom_fusion.2, s32[2304]{0:T(1024)S(1)} %get-tuple-element.20, bf16[2304,512]{1,0:T(8,128)(2,1)} %get-tuple-element.27), kind=kCustom, calls=%fused_computation.11 | custom fusion | flops 2359296 | bytes 4980736 | tf_op jit(solution)/shard_map/scatter-add | solution.py:86
  269.4 0.0 copy-start.2
  269.4 1.5 copy-done.2
  270.9 0.0 reduce-scatter.2.cloned.1.call-update
  270.9 0.3 all-reduce.3.cloned.1.call-start
  271.2 4.8 %fusion.24 = f32[512,512]{0,1:T(8,128)} fusion(bf16[2304,512]{1,0:T(8,128)(2,1)} %get-tuple-element.29, bf16[2304,512]{1,0:T(8,128)(2,1)} %copy-done.5), kind=kOutput, calls=%fused_computation.74 | convolution fusion | flops 1207959552 | bytes 5767168 | tf_op jit(solution)/shard_map/dot_general | solution.py:19
  275.9 5.0 %fusion.12 = f32[512,227]{0,1:T(8,128)} fusion(bf16[2304,739]{1,0:T(8,128)(2,1)} %bitcast.2, bf16[2304,512]{1,0:T(8,128)(2,1)} %get-tuple-element.29, bf16[512,512]{1,0:T(8,128)(2,1)S(1)} %copy-done), kind=kOutput, calls=%fused_computation.37 | convolution fusion | flops 1744699392 | bytes 4528128 | tf_op jit(solution)/shard_map/dot_general | solution.py:19
  280.9 5.5 %fusion.7 = f32[512,512]{0,1:T(8,128)} fusion(bf16[2304,512]{1,0:T(8,128)(2,1)} %get-tuple-element.27, bf16[2304,512]{1,0:T(8,128)(2,1)} %get-tuple-element.28, bf16[2304,512]{1,0:T(8,128)(2,1)S(1)} %copy-done.4, bf16[2304,739]{1,0:T(8,128)(2,1)} %bitcast.2), kind=kOutput, calls=%fused_computation.29 | convolution fusion | flops 1215037440 | bytes 10485760 | tf_op jit(solution)/shard_map/dot_general | solution.py:19
  286.5 19.3 %reduce-scatter.2.cloned.1.call-done = f32[320,512]{1,0:T(8,128)} async-done(((f32[1280,512]{1,0:T(8,128)}), f32[320,512]{1,0:T(8,128)}) %reduce-scatter.2.cloned.1.call-update) | async-done | bytes 655376 | tf_op jit(solution)/shard_map/reduce_scatter | solution.py:87
  305.8 2.6 convolution_bitcast_fusion
  308.4 0.0 all-reduce.3.cloned.1.call-update
  308.4 1.1 convolution_convert_fusion.3
  309.5 143.8 %all-reduce.3.cloned.1.call-done = (f32[512,512]{0,1:T(8,128)}, f32[512,512]{0,1:T(8,128)}, f32[512,512]{0,1:T(8,128)}, f32[512,227]{0,1:T(8,128)}) async-done(((f32[512,512]{0,1:T(8,128)}, f32[512,512]{0,1:T(8,128)}, f32[512,512]{0,1:T(8,128)}, f32[512,227]{0,1:T(8,128)}), (f32[512,512]{0,1:T(8,128)}, f32[512,512]{0,1:T(8,128)}, f32[512,512]{0,1:T(8,128)}, ...) | async-done | bytes 3610640 | tf_op jit(solution)/shard_map/psum | solution.py:94
  453.3 1.4 broadcast_multiply_fusion.2
  454.7 1.3 copy.29
  456.0 0.8 broadcast_multiply_fusion.3
  456.8 1.3 broadcast_multiply_fusion.1
  458.2 1.3 copy.30
  459.5 0.1 broadcast_multiply_fusion
  459.6 1.3 copy.31
  (31 shorter events, 0.1 us)
Async XLA Ops:
  7.2 200.5 %copy-start = (bf16[512,512]{1,0:T(8,128)(2,1)S(1)}, bf16[512,512]{1,0:T(8,128)(2,1)}, u32[]{:S(2)}) copy-start(bf16[512,512]{1,0:T(8,128)(2,1)} %param.16) | copy-start | bytes 1572868
  114.1 7.5 %copy-start.9 = (bf16[512,512]{1,0:T(8,128)(2,1)S(1)}, bf16[512,512]{1,0:T(8,128)(2,1)}, u32[]{:S(2)}) copy-start(bf16[512,512]{1,0:T(8,128)(2,1)} %param.14) | copy-start | bytes 1572868
  114.1 7.5 %copy-start.11 = (bf16[320,512]{1,0:T(8,128)(2,1)S(1)}, bf16[320,512]{1,0:T(8,128)(2,1)}, u32[]{:S(2)}) copy-start(bf16[320,512]{1,0:T(8,128)(2,1)} %param.11) | copy-start | bytes 983044
  114.1 8.7 %copy-start.15 = (s32[3,2304]{1,0:T(4,128)S(1)}, s32[3,2304]{1,0:T(4,128)}, u32[]{:S(2)}) copy-start(s32[3,2304]{1,0:T(4,128)} %param.13) | copy-start | bytes 82948
  114.1 87.5 %all-to-all-start = ((bf16[32,72,739]{2,1,0:T(8,128)(2,1)}), bf16[32,72,739]{2,1,0:T(8,128)(2,1)}, u32[]{:S(2)}, u32[]{:S(2)}) async-start(bf16[32,72,739]{2,1,0:T(8,128)(2,1)} %scatter_fusion), calls=%async_computation | async-start | bytes 7077888 | tf_op jit(solution)/shard_map/all_to_all | solution.py:49
  121.6 35.3 %all-gather.2.cloned.1.call-start = ((), (), s32[]{:S(2)}) async-start(), calls=%async_computation.2 | async-start | bytes 1638400 | tf_op jit(solution)/shard_map/all_gather | solution.py:60
  122.7 183.0 %reduce-scatter.2.cloned.1.call-start = ((), (), s32[]{:S(2)}) async-start(), calls=%async_computation.3 | async-start | bytes 3276800 | tf_op jit(solution)/shard_map/reduce_scatter | solution.py:87
  156.9 9.2 %copy-start.1 = (bf16[1280,512]{1,0:T(8,128)(2,1)S(1)}, bf16[1280,512]{1,0:T(8,128)(2,1)}, u32[]{:S(2)}) copy-start(bf16[1280,512]{1,0:T(8,128)(2,1)} %all-gather.2.cloned.1.call-done) | copy-start | bytes 3932164
  173.6 28.0 %copy-start.14 = (bf16[512,227]{0,1:T(8,128)(2,1)S(1)}, bf16[512,227]{0,1:T(8,128)(2,1)}, u32[]{:S(2)}) copy-start(bf16[512,227]{0,1:T(8,128)(2,1)} %param.17) | copy-start | bytes 697348
  181.1 22.6 %copy-start.16 = (bf16[512,512]{1,0:T(8,128)(2,1)S(1)}, bf16[512,512]{1,0:T(8,128)(2,1)}, u32[]{:S(2)}) copy-start(bf16[512,512]{1,0:T(8,128)(2,1)} %param.15) | copy-start | bytes 1572868
  203.7 4.0 copy-start.5
  203.7 4.0 copy-start.6
  203.7 4.0 copy-start.7
  203.7 4.6 copy-start.8
  269.4 1.5 copy-start.2
  270.9 182.4 %all-reduce.3.cloned.1.call-start = ((), (), s32[]{:S(2)}) async-start(), calls=%async_computation.4 | async-start | bytes 7241728 | tf_op jit(solution)/shard_map/psum | solution.py:94
  275.9 5.0 %copy-start.4 = (bf16[2304,512]{1,0:T(8,128)(2,1)S(1)}, bf16[2304,512]{1,0:T(8,128)(2,1)}, u32[]{:S(2)}) copy-start(bf16[2304,512]{1,0:T(8,128)(2,1)} %get-tuple-element.30) | copy-start | bytes 7077892
  286.5 21.9 %copy-start.10 = (bf16[512,512]{1,0:T(8,128)(2,1)S(1)}, bf16[512,512]{1,0:T(8,128)(2,1)}, u32[]{:S(2)}) copy-start(bf16[512,512]{1,0:T(8,128)(2,1)} %param.14) | copy-start | bytes 1572868
  305.8 2.6 copy-start.3
  453.3 2.7 copy-start.13
  456.0 3.5 copy-start.12
Sparse Core Ops, SparseCore 0:
  124.5 32.3 all-gather.1
  271.0 34.7 reduce-scatter.1
  312.4 140.8 all-reduce.2
where the time goes:
time: 472 us; the launch traced here: 467 us
  waiting for transfers between devices  218 us (46%)
  local copies, waits for them, and re-layouts  134 us (28%)
  other arithmetic  58.8 us (12%)
  matrix products  35.1 us (7%)
  between operations  14 us (3%)
  starting transfers between devices  7.79 us (2%)
    psum x1, waiting for transfers between devices, shards(): mesh_total = lax.psum(mesh_part, ('band', 'sub'))  144 us
    scatter x1, local copies, waits for them, and re-layouts, shards(): jnp.zeros((devices, capacity, row_width), jnp.bfloat16)  102 us
    scatter-add x3, other arithmetic, shards(): node_part.at[local_node[corner]].add(pre_grads[corner].astype(jnp.float32))  51.9 us
    all_gather x1, waiting for transfers between devices, shards(): patch_proj = lax.all_gather(mesh_proj, 'sub', axis=0, tiled=True)  33.9 us
    gather x3, local copies, waits for them, and re-layouts, shards(): patch_proj[local_node[corner]].astype(jnp.float32) + grid_float  24.2 us
    all_to_all x1, waiting for transfers between devices, shards(): lax.all_to_all(send_buffer, ('band', 'sub'), split_axis=0, concat_axis=0,...  20.5 us
    reduce_scatter x1, waiting for transfers between devices, shards(): lax.psum_scatter(node_part, 'sub', scatter_dimension=0, tiled=True)  19.3 us
    dot_general x4, matrix products, contract_rows(): lax.dot_general(left, right, (((0,), (0,)), ((), ())), preferred_element_...  17.9 us
  transfers between devices with their start and end apart: 4, of which 4 were waited for; matrix products, arithmetic and copies ran while one was open for 9% of the time, Pallas kernels for 0%

commit v1 on v0

--- a/solution.py
+++ b/solution.py
@@ -91,7 +91,7 @@
     mesh_part = contract_rows(mesh_latent, mesh_proj_grad)
     grad_scale = 1.0 / math.sqrt(3.0 * total_points)
     grid_total = lax.psum(grid_part, ("band", "sub"))
-    mesh_total = lax.psum(mesh_part, ("band", "sub"))
+    mesh_total = lax.psum(lax.psum(mesh_part, "sub"), "band")
     return (
         mesh_grad,
         mesh_total * grad_scale,

time: 472 us -> 583 us (1.24)
  waiting for transfers between devices: 218 us -> 328 us
    psum x1 -> x3, waiting for transfers between devices: 144 us -> 245 us  [the longest x1 144 us: shards(): grid_total = lax.psum(grid_part, ('band', 'sub'))]
    reduce_scatter x1, waiting for transfers between devices: 19.3 us -> 28.6 us  [shards(): lax.psum_scatter(node_part, 'sub', scatter_dimension=0, tiled=True)]
  transfers between devices with their start and end apart: 4 -> 6, of which waited for: 4 -> 6; matrix products, arithmetic and copies ran while one was open for 9% -> 8% of each run, Pallas kernels for 0% -> 0%
where the time goes in v1:
time: 583 us; the launch traced here: 579 us
  waiting for transfers between devices  328 us (56%)
  local copies, waits for them, and re-layouts  134 us (23%)
  other arithmetic  60.1 us (10%)
  matrix products  34.8 us (6%)
  between operations  14 us (2%)
  starting transfers between devices  7.7 us (1%)
    psum x1, waiting for transfers between devices, shards(): grid_total = lax.psum(grid_part, ('band', 'sub'))  144 us
    scatter x1, local copies, waits for them, and re-layouts, shards(): jnp.zeros((devices, capacity, row_width), jnp.bfloat16)  101 us
    psum x2, waiting for transfers between devices, shards(): mesh_total = lax.psum(lax.psum(mesh_part, 'sub'), 'band')  101 us
    scatter-add x3, other arithmetic, shards(): node_part.at[local_node[corner]].add(pre_grads[corner].astype(jnp.float32))  51.9 us
    all_gather x1, waiting for transfers between devices, shards(): patch_proj = lax.all_gather(mesh_proj, 'sub', axis=0, tiled=True)  33.9 us
    reduce_scatter x1, waiting for transfers between devices, shards(): lax.psum_scatter(node_part, 'sub', scatter_dimension=0, tiled=True)  28.6 us
    gather x3, local copies, waits for them, and re-layouts, shards(): patch_proj[local_node[corner]].astype(jnp.float32) + grid_float  24.2 us
    all_to_all x1, waiting for transfers between devices, shards(): lax.all_to_all(send_buffer, ('band', 'sub'), split_axis=0, concat_axis=0,...  20.5 us
  transfers between devices with their start and end apart: 6, of which 6 were waited for; matrix products, arithmetic and copies ran while one was open for 8% of the time, Pallas kernels for 0%

profile of v1, /device:TPU:0, one launch (start us, length us, event | category | flops | bytes accessed | tf_op | source)
XLA Modules:
  0.0 579.0 jit_solution(12901763216712008063)
XLA Ops:
  7.2 0.8 compare_select_fusion.4
  8.0 1.0 fusion.15
  9.0 0.2 copy.26
  9.2 1.2 pad_maximum_fusion
  10.5 2.0 broadcast_in_dim.9
  12.5 101.4 %scatter_fusion = bf16[32,72,739]{2,1,0:T(8,128)(2,1)} fusion(bf16[32,72,739]{2,1,0:T(8,128)(2,1)} %broadcast_in_dim.9, s32[768]{0:T(1024)S(1)} %fusion.23, bf16[768,739]{1,0:T(8,128)(2,1)S(1)} %pad_maximum_fusion), kind=kCustom, calls=%fused_computation.3 | custom fusion | bytes 3411456 | tf_op jit(solution)/shard_map/scatter | solution.py:47
  114.0 7.5 %all-to-all-start = ((bf16[32,72,739]{2,1,0:T(8,128)(2,1)}), bf16[32,72,739]{2,1,0:T(8,128)(2,1)}, u32[]{:S(2)}, u32[]{:S(2)}) async-start(bf16[32,72,739]{2,1,0:T(8,128)(2,1)} %scatter_fusion), calls=%async_computation | async-start | bytes 7077888 | tf_op jit(solution)/shard_map/all_to_all | solution.py:49
  121.5 0.0 all-gather.2.cloned.1.call-start
  121.5 1.1 convolution_convert_fusion.4
  122.6 0.0 all-gather.2.cloned.1.call-update
  122.6 0.0 reduce-scatter.2.cloned.1.call-start
  122.7 0.1 fusion.20
  122.8 33.9 %all-gather.2.cloned.1.call-done = bf16[1280,512]{1,0:T(8,128)(2,1)} async-done(((bf16[320,512]{1,0:T(8,128)(2,1)}), bf16[1280,512]{1,0:T(8,128)(2,1)}) %all-gather.2.cloned.1.call-update) | async-done | bytes 1310736 | tf_op jit(solution)/shard_map/all_gather | solution.py:60
  156.8 9.2 %gather_fusion.2 = bf16[2304,512]{1,0:T(8,128)(2,1)} fusion(bf16[1280,512]{1,0:T(8,128)(2,1)} %all-gather.2.cloned.1.call-done, s32[3072]{0:T(1024)S(1)} %get-tuple-element.32), kind=kCustom, calls=%fused_computation.2 | custom fusion | bytes 4727808 | tf_op jit(solution)/shard_map/gather | solution.py:66
  166.0 7.5 %gather_fusion.1 = bf16[2304,512]{1,0:T(8,128)(2,1)} fusion(bf16[1280,512]{1,0:T(8,128)(2,1)S(1)} %copy-done.1, s32[3072]{0:T(1024)S(1)} %get-tuple-element.33), kind=kCustom, calls=%fused_computation.1 | custom fusion | bytes 4727808 | tf_op jit(solution)/shard_map/gather | solution.py:66
  173.5 7.5 %gather_fusion = bf16[2304,512]{1,0:T(8,128)(2,1)} fusion(bf16[1280,512]{1,0:T(8,128)(2,1)S(1)} %copy-done.1, s32[3072]{0:T(1024)S(1)} %pad_clamp_fusion.2), kind=kCustom, calls=%fused_computation | custom fusion | bytes 4727808 | tf_op jit(solution)/shard_map/gather | solution.py:66
  181.0 20.5 %all-to-all-done = bf16[32,72,739]{2,1,0:T(8,128)(2,1)} async-done(((bf16[32,72,739]{2,1,0:T(8,128)(2,1)}), bf16[32,72,739]{2,1,0:T(8,128)(2,1)}, u32[]{:S(2)}, u32[]{:S(2)}) %all-to-all-start) | async-done | bytes 3405344 | tf_op jit(solution)/shard_map/all_to_all | solution.py:49
  201.5 2.0 convolution_convert_fusion.2
  203.6 3.9 convolution_convert_fusion.1
  207.6 0.6 copy-done.8
  208.2 9.1 %multiply_convert_fusion = (bf16[2304,512]{1,0:T(8,128)(2,1)}, bf16[2304,512]{1,0:T(8,128)(2,1)}, bf16[2304,512]{1,0:T(8,128)(2,1)}, bf16[2304,512]{1,0:T(8,128)(2,1)}) fusion(bf16[2304,512]{1,0:T(8,128)(2,1)S(1)} %convolution_convert_fusion.1, bf16[2304,512]{1,0:T(8,128)(2,1)S(1)} %copy-done.6, bf16[2304,512]{1,0:T(8,128)(2,1)S(1)} %copy-done.7, ...), kind=kOutput, calls=%fused_computation.20 | convolution fusion | flops 1255145472 | bytes 21757952 | tf_op jit(solution)/shard_map/dot_general | solution.py:25
  217.3 17.0 %scatter_custom_fusion.1 = f32[1280,512]{1,0:T(8,128)S(1)} fusion(s32[2304]{0:T(1024)S(1)} %get-tuple-element.22, bf16[2304,512]{1,0:T(8,128)(2,1)} %get-tuple-element.29, f32[]{:T(128)} %constant.20.clone.1), kind=kCustom, calls=%fused_computation.16 | custom fusion | flops 2359296 | bytes 4980740 | tf_op jit(solution)/shard_map/scatter-add | solution.py:86
  234.3 17.5 %scatter_custom_fusion.2 = f32[1280,512]{1,0:T(8,128)S(1)} fusion(f32[1280,512]{1,0:T(8,128)S(1)} %scatter_custom_fusion.1, s32[2304]{0:T(1024)S(1)} %get-tuple-element.21, bf16[2304,512]{1,0:T(8,128)(2,1)} %get-tuple-element.27), kind=kCustom, calls=%fused_computation.14 | custom fusion | flops 2359296 | bytes 4980736 | tf_op jit(solution)/shard_map/scatter-add | solution.py:86
  251.9 17.4 %scatter_custom_fusion.3 = f32[1280,512]{1,0:T(8,128)S(1)} fusion(f32[1280,512]{1,0:T(8,128)S(1)} %scatter_custom_fusion.2, s32[2304]{0:T(1024)S(1)} %get-tuple-element.20, bf16[2304,512]{1,0:T(8,128)(2,1)} %get-tuple-element.26), kind=kCustom, calls=%fused_computation.11 | custom fusion | flops 2359296 | bytes 4980736 | tf_op jit(solution)/shard_map/scatter-add | solution.py:86
  269.2 1.5 copy-done.2
  270.7 0.0 reduce-scatter.2.cloned.1.call-update
  270.8 0.0 all-reduce.5.cloned.1.call-start
  270.8 6.2 %fusion.7 = f32[512,512]{0,1:T(8,128)} fusion(bf16[2304,512]{1,0:T(8,128)(2,1)} %get-tuple-element.26, bf16[2304,512]{1,0:T(8,128)(2,1)} %get-tuple-element.27, bf16[2304,512]{1,0:T(8,128)(2,1)} %get-tuple-element.29, bf16[2304,739]{1,0:T(8,128)(2,1)} %bitcast.2), kind=kOutput, calls=%fused_computation.29 | convolution fusion | flops 1215037440 | bytes 10485760 | tf_op jit(solution)/shard_map/dot_general | solution.py:19
  277.0 28.6 %reduce-scatter.2.cloned.1.call-done = f32[320,512]{1,0:T(8,128)} async-done(((f32[1280,512]{1,0:T(8,128)}), f32[320,512]{1,0:T(8,128)}) %reduce-scatter.2.cloned.1.call-update) | async-done | bytes 655376 | tf_op jit(solution)/shard_map/reduce_scatter | solution.py:87
  305.7 2.5 convolution_bitcast_fusion
  308.2 0.0 all-reduce.5.cloned.1.call-update
  308.2 0.0 all-reduce.9.cloned.1.call-start
  308.3 4.1 fusion.24
  312.3 4.9 fusion.12
  317.2 0.0 all-reduce.9.cloned.1.call-update
  317.2 0.0 all-reduce.7.cloned.1.call-start
  317.3 27.7 %all-reduce.5.cloned.1.call-done = f32[512,512]{0,1:T(8,128)} async-done(((f32[512,512]{0,1:T(8,128)}), f32[512,512]{0,1:T(8,128)}) %all-reduce.5.cloned.1.call-update) | async-done | bytes 1048592 | tf_op jit(solution)/shard_map/psum | solution.py:94
  345.0 0.0 all-reduce.7.cloned.1.call-update
  345.0 143.9 %all-reduce.9.cloned.1.call-done = (f32[512,512]{0,1:T(8,128)}, f32[512,512]{0,1:T(8,128)}, f32[512,227]{0,1:T(8,128)}) async-done(((f32[512,512]{0,1:T(8,128)}, f32[512,512]{0,1:T(8,128)}, f32[512,227]{0,1:T(8,128)}), (f32[512,512]{0,1:T(8,128)}, f32[512,512]{0,1:T(8,128)}, f32[512,227]{0,1:T(8,128)})) %all-reduce.9.cloned.1.call-update) | async-done | bytes 2562064 | tf_op jit(solution)/shard_map/psum | solution.py:93
  488.9 1.3 broadcast_multiply_fusion.1
  490.2 1.3 copy.30
  491.5 1.5 broadcast_multiply_fusion
  493.0 1.3 copy.31
  494.3 0.8 broadcast_multiply_fusion.3
  495.1 1.1 convolution_convert_fusion.3
  496.2 73.6 %all-reduce.7.cloned.1.call-done = f32[512,512]{0,1:T(8,128)} async-done(((f32[512,512]{0,1:T(8,128)}), f32[512,512]{0,1:T(8,128)}) %all-reduce.7.cloned.1.call-update) | async-done | bytes 1048592 | tf_op jit(solution)/shard_map/psum | solution.py:94
  569.8 1.3 broadcast_multiply_fusion.2
  571.1 1.3 copy.29
  (35 shorter events, 0.2 us)
Async XLA Ops:
  7.2 200.4 %copy-start = (bf16[512,512]{1,0:T(8,128)(2,1)S(1)}, bf16[512,512]{1,0:T(8,128)(2,1)}, u32[]{:S(2)}) copy-start(bf16[512,512]{1,0:T(8,128)(2,1)} %param.16) | copy-start | bytes 1572868
  113.9 7.6 %copy-start.9 = (bf16[512,512]{1,0:T(8,128)(2,1)S(1)}, bf16[512,512]{1,0:T(8,128)(2,1)}, u32[]{:S(2)}) copy-start(bf16[512,512]{1,0:T(8,128)(2,1)} %param.14) | copy-start | bytes 1572868
  113.9 7.6 %copy-start.11 = (bf16[320,512]{1,0:T(8,128)(2,1)S(1)}, bf16[320,512]{1,0:T(8,128)(2,1)}, u32[]{:S(2)}) copy-start(bf16[320,512]{1,0:T(8,128)(2,1)} %param.11) | copy-start | bytes 983044
  113.9 8.7 %copy-start.14 = (s32[3,2304]{1,0:T(4,128)S(1)}, s32[3,2304]{1,0:T(4,128)}, u32[]{:S(2)}) copy-start(s32[3,2304]{1,0:T(4,128)} %param.13) | copy-start | bytes 82948
  114.0 87.6 %all-to-all-start = ((bf16[32,72,739]{2,1,0:T(8,128)(2,1)}), bf16[32,72,739]{2,1,0:T(8,128)(2,1)}, u32[]{:S(2)}, u32[]{:S(2)}) async-start(bf16[32,72,739]{2,1,0:T(8,128)(2,1)} %scatter_fusion), calls=%async_computation | async-start | bytes 7077888 | tf_op jit(solution)/shard_map/all_to_all | solution.py:49
  121.5 35.3 %all-gather.2.cloned.1.call-start = ((), (), s32[]{:S(2)}) async-start(), calls=%async_computation.2 | async-start | bytes 1638400 | tf_op jit(solution)/shard_map/all_gather | solution.py:60
  122.6 183.1 %reduce-scatter.2.cloned.1.call-start = ((), (), s32[]{:S(2)}) async-start(), calls=%async_computation.3 | async-start | bytes 3276800 | tf_op jit(solution)/shard_map/reduce_scatter | solution.py:87
  156.8 9.2 %copy-start.1 = (bf16[1280,512]{1,0:T(8,128)(2,1)S(1)}, bf16[1280,512]{1,0:T(8,128)(2,1)}, u32[]{:S(2)}) copy-start(bf16[1280,512]{1,0:T(8,128)(2,1)} %all-gather.2.cloned.1.call-done) | copy-start | bytes 3932164
  173.5 28.0 %copy-start.13 = (bf16[512,227]{0,1:T(8,128)(2,1)S(1)}, bf16[512,227]{0,1:T(8,128)(2,1)}, u32[]{:S(2)}) copy-start(bf16[512,227]{0,1:T(8,128)(2,1)} %param.17) | copy-start | bytes 697348
  181.0 22.6 %copy-start.15 = (bf16[512,512]{1,0:T(8,128)(2,1)S(1)}, bf16[512,512]{1,0:T(8,128)(2,1)}, u32[]{:S(2)}) copy-start(bf16[512,512]{1,0:T(8,128)(2,1)} %param.15) | copy-start | bytes 1572868
  203.6 4.0 copy-start.4
  203.6 4.0 copy-start.6
  203.6 4.0 copy-start.7
  203.6 4.6 copy-start.8
  269.2 1.5 copy-start.2
  270.8 74.2 %all-reduce.5.cloned.1.call-start = ((), (), s32[]{:S(2)}) async-start(), calls=%async_computation.4 | async-start | bytes 2097152 | tf_op jit(solution)/shard_map/psum | solution.py:94
  277.0 31.2 %copy-start.5 = (bf16[2304,512]{1,0:T(8,128)(2,1)S(1)}, bf16[2304,512]{1,0:T(8,128)(2,1)}, u32[]{:S(2)}) copy-start(bf16[2304,512]{1,0:T(8,128)(2,1)} %copy-done.4) | copy-start | bytes 7077892
  308.2 180.7 %all-reduce.9.cloned.1.call-start = ((), (), s32[]{:S(2)}) async-start(), calls=%async_computation.6 | async-start | bytes 5144576 | tf_op jit(solution)/shard_map/psum | solution.py:93
  317.2 252.6 %all-reduce.7.cloned.1.call-start = ((), (), s32[]{:S(2)}) async-start(), calls=%async_computation.5 | async-start | bytes 2097152 | tf_op jit(solution)/shard_map/psum | solution.py:94
  491.5 2.8 copy-start.12
  491.5 3.6 copy-start.3
  491.5 3.6 copy-start.10
Sparse Core Ops, SparseCore 0:
  124.4 32.3 all-gather.1
  270.9 34.7 reduce-scatter.1
  308.6 36.2 all-reduce.4
  351.3 137.5 all-reduce.8
  492.2 77.5 all-reduce.6
